TPU v7x, 32 devices: a whole 2x2x4 slice. The times are simulated.
32 devices in a mesh: freq: 8 (over z, y), cell: 4 (over x, core).
Axes of the slice: x: 2, y: 2, z: 4, core: 2. Of those that a mesh axis runs over, the one named last changes fastest.
Arguments:
- columns: float32 [2, 16, 64, 600], P(None, 'freq'), may hold values from -6 to 6
- freq_blocks: float32 [2, 16, 600, 1024], P(None, 'freq', None, 'cell'), may hold values from -0.1875 to 0.1875
- causal_cutoffs: int32 [64], replicated, may hold values from 3 to 15
- band_index: int32 [1024], P('cell'), may hold values from 0 to 7
- band_rates: float32 [8], replicated, may hold values from 0.05 to 0.45
Outputs:
- hessian_columns: float32 [2, 16, 64, 600], P(None, 'freq', 'cell')
All inputs are finite; a program needn't handle non-finite values.
Results may differ from a plain program's by a relative error of at most 0.00007.
Values sent between devices are 32-bit elements; how exact they have to be, the bound alone decides.
No kernel may reach another device: no remote copies, remote signals or barrier semaphores. Data moves between devices by JAX's collectives and lax.ppermute only.
A program may use at most 64 MiB of HBM per device.

v0:
```python
import math
import jax
import jax.numpy as jnp
from jax import lax
from jax.sharding import PartitionSpec as P

MODE_SHARE_WIDTH = 8
C_DEV = 256
SWEEPS = 4
BANDS = 8
precise = lax.Precision.HIGHEST


def extended(shard, sides, width):
    for axis, dim in sides:
        devices, length = (lax.axis_size(axis), shard.shape[dim])
        up = [(i, (i + 1) % devices) for i in range(devices - 1)]
        down = [(j, i) for i, j in up]
        last = lax.slice_in_dim(shard, length - width, length, axis=dim)
        leading = lax.slice_in_dim(shard, 0, width, axis=dim)
        before = lax.ppermute(last, axis, up)
        after = lax.ppermute(leading, axis, down)
        shard = jnp.concatenate([before, shard, after], axis=dim)
    return shard


def inverse_table(epoch_number, harmonic_number):
    cycle_length = 2 * epoch_number
    sample_moments = lax.broadcasted_iota(jnp.int32, (epoch_number, harmonic_number), 0)
    harmonic_rate = lax.broadcasted_iota(jnp.int32, (epoch_number, harmonic_number), 1)
    harmonic_offsets = (sample_moments * harmonic_rate % cycle_length).astype(jnp.float32) * (
        2.0 * math.pi / cycle_length
    )
    weight = (
        jnp.where((harmonic_rate == 0) | (harmonic_rate == harmonic_number - 1), 1.0, 2.0).astype(
            jnp.float32
        )
        / cycle_length
    )
    return jnp.concatenate(
        [weight * jnp.cos(harmonic_offsets), -weight * jnp.sin(harmonic_offsets)], axis=1
    )


def forward_table(epoch_number, harmonic_number):
    cycle_length = 2 * epoch_number
    harmonic_rate = lax.broadcasted_iota(jnp.int32, (harmonic_number, epoch_number), 0)
    sample_moments = lax.broadcasted_iota(jnp.int32, (harmonic_number, epoch_number), 1)
    harmonic_offsets = (sample_moments * harmonic_rate % cycle_length).astype(jnp.float32) * (
        2.0 * math.pi / cycle_length
    )
    return jnp.concatenate([jnp.cos(harmonic_offsets), -jnp.sin(harmonic_offsets)], axis=0)


def adjoint_product(columns, blocks):
    real_part = jnp.einsum("kjs,ksm->kjm", columns[0], blocks[0], precision=precise) + jnp.einsum(
        "kjs,ksm->kjm", columns[1], blocks[1], precision=precise
    )
    imag_part = jnp.einsum("kjs,ksm->kjm", columns[1], blocks[0], precision=precise) - jnp.einsum(
        "kjs,ksm->kjm", columns[0], blocks[1], precision=precise
    )
    return jnp.stack([real_part, imag_part])


def forward_product(spectrum, blocks):
    real_part = jnp.einsum("kjm,ksm->kjs", spectrum[0], blocks[0], precision=precise) - jnp.einsum(
        "kjm,ksm->kjs", spectrum[1], blocks[1], precision=precise
    )
    imag_part = jnp.einsum("kjm,ksm->kjs", spectrum[1], blocks[0], precision=precise) + jnp.einsum(
        "kjm,ksm->kjs", spectrum[0], blocks[1], precision=precise
    )
    return jnp.stack([real_part, imag_part])


def on_device(columns, freq_blocks, causal_cutoffs, band_index, band_rates):
    col_total = columns.shape[2]
    local_spectrum = adjoint_product(columns, freq_blocks)
    gathered = lax.all_to_all(local_spectrum, "freq", split_axis=2, concat_axis=1, tiled=True)
    freq_total = gathered.shape[1]
    horizon_span = freq_total - 1
    sampled_trace = jnp.dot(
        inverse_table(horizon_span, freq_total),
        gathered.reshape(2 * freq_total, MODE_SHARE_WIDTH * C_DEV),
        precision=precise,
        preferred_element_type=jnp.float32,
    )
    sampled_trace = sampled_trace.reshape(horizon_span, MODE_SHARE_WIDTH, C_DEV)
    device_ranges = lax.dynamic_slice_in_dim(
        causal_cutoffs, lax.axis_index("freq") * MODE_SHARE_WIDTH, MODE_SHARE_WIDTH
    )
    sample_moments = lax.broadcasted_iota(jnp.int32, (horizon_span, MODE_SHARE_WIDTH), 0)
    sampled_trace = jnp.where(
        (sample_moments < device_ranges[None, :])[:, :, None], sampled_trace, 0.0
    )
    flat = sampled_trace.reshape(horizon_span * MODE_SHARE_WIDTH, C_DEV)
    levels = lax.broadcasted_iota(jnp.int32, (BANDS, C_DEV), 0)
    cell_rates = jnp.sum(jnp.where(levels == band_index[None, :], band_rates[:, None], 0.0), axis=0)
    stacked = jnp.concatenate([flat, cell_rates[None, :]], axis=0)
    padded = extended(stacked, (("cell", 1),), SWEEPS)
    field = padded[:-1]
    margin_rates = padded[-1]
    for repeat in range(SWEEPS):
        inner_rates = margin_rates[1:-1]
        field = field[:, 1:-1] + inner_rates * (field[:, :-2] - 2.0 * field[:, 1:-1] + field[:, 2:])
        margin_rates = inner_rates
    flat = field
    spectrum = jnp.dot(
        forward_table(horizon_span, freq_total),
        flat.reshape(horizon_span, MODE_SHARE_WIDTH * C_DEV),
        precision=precise,
        preferred_element_type=jnp.float32,
    )
    spectrum = spectrum.reshape(2, freq_total, MODE_SHARE_WIDTH, C_DEV)
    returned = lax.all_to_all(spectrum, "freq", split_axis=1, concat_axis=2, tiled=True)
    partial_terms = forward_product(returned, freq_blocks)
    totals = lax.psum(partial_terms, "cell")
    share = col_total // lax.axis_size("cell")
    return lax.dynamic_slice_in_dim(totals, lax.axis_index("cell") * share, share, 2)


def solution(mesh):
    placed = (P(None, "freq", None, None), P(None, "freq", None, "cell"), P(), P("cell"), P())
    return jax.shard_map(
        on_device,
        mesh=mesh,
        in_specs=placed,
        out_specs=P(None, "freq", "cell", None),
        check_vma=False,
    )
```

profile of v0, /device:TPU:0, one launch (start us, length us, event | category | flops | bytes accessed | tf_op | source)
XLA Modules:
  0.0 98.5 jit_solution(15903029011630750266)
XLA Ops:
  6.5 2.4 %fusion.4 = f32[2,64,256]{2,1,0:T(8,128)S(1)} fusion(f32[2,2,600,256]{3,2,1,0:T(8,128)} %param.6, f32[2,2,64,600]{3,2,1,0:T(8,128)} %param.5), kind=kOutput, calls=%fused_computation.4 | convolution fusion | flops 235929600 | bytes 1687552 | tf_op jit(solution)/shard_map/kjs,ksm->kjm/dot_general | solution.py:59
  9.0 2.3 %fusion.6 = f32[2,64,256]{2,1,0:T(8,128)S(1)} fusion(f32[2,2,600,256]{3,2,1,0:T(8,128)} %param.6, f32[2,2,64,600]{3,2,1,0:T(8,128)} %param.5), kind=kOutput, calls=%fused_computation.6 | convolution fusion | flops 235929600 | bytes 1687552 | tf_op jit(solution)/shard_map/kjs,ksm->kjm/dot_general | solution.py:56
  11.4 0.9 fusion.37
  12.3 0.9 fusion.31
  13.2 0.9 copy.21
  14.1 7.3 %all-to-all-start = ((f32[2,2,64,256]{3,1,0,2:T(2,128)}), f32[2,2,64,256]{3,1,0,2:T(2,128)S(1)}, u32[]{:S(2)}, u32[]{:S(2)}) async-start(f32[2,2,64,256]{3,1,0,2:T(2,128)} %copy.21), calls=%async_computation | async-start | bytes 524288 | tf_op jit(solution)/shard_map/all_to_all | solution.py:78
  21.6 0.1 select_reduce_fusion
  21.6 0.1 dynamic_slice.6
  21.9 8.5 %all-to-all-done = f32[2,2,64,256]{3,1,0,2:T(2,128)S(1)} async-done(((f32[2,2,64,256]{3,1,0,2:T(2,128)}), f32[2,2,64,256]{3,1,0,2:T(2,128)S(1)}, u32[]{:S(2)}, u32[]{:S(2)}) %all-to-all-start) | async-done | bytes 262176 | tf_op jit(solution)/shard_map/all_to_all | solution.py:78
  30.4 0.3 convolution_select_fusion
  30.8 0.1 fusion.69
  30.9 1.3 %collective-permute-start = (f32[121,4]{1,0:T(8,128)S(1)}, f32[121,4]{1,0:T(8,128)S(1)}, u32[]{:S(2)}, u32[]{:S(2)}) collective-permute-start(f32[121,4]{1,0:T(8,128)S(1)} %get-tuple-element.5), channel_id=1, source_target_pairs={{0,1},{1,2},{2,3},{4,5},{5,6},{6,7},{8,9},{9,10},{10,11},{12,13},{... | collective-permute-start | bytes 5816 | tf_op jit(solution)/shard_map/ppermute | solution.py:21
  32.2 1.3 %collective-permute-start.1 = (f32[121,4]{1,0:T(8,128)S(1)}, f32[121,4]{1,0:T(8,128)S(1)}, u32[]{:S(2)}, u32[]{:S(2)}) collective-permute-start(f32[121,4]{1,0:T(8,128)S(1)} %get-tuple-element.6), channel_id=1, source_target_pairs={{1,0},{2,1},{3,2},{5,4},{6,5},{7,6},{9,8},{10,9},{11,10},{13,12},{... | collective-permute-start | bytes 5816 | tf_op jit(solution)/shard_map/ppermute | solution.py:22
  33.5 3.5 %collective-permute-done.1 = f32[121,4]{1,0:T(8,128)S(1)} collective-permute-done((f32[121,4]{1,0:T(8,128)S(1)}, f32[121,4]{1,0:T(8,128)S(1)}, u32[]{:S(2)}, u32[]{:S(2)}) %collective-permute-start.1) | collective-permute-done | bytes 1968 | tf_op jit(solution)/shard_map/ppermute | solution.py:22
  37.1 0.1 maximum_reduce_fusion.2
  37.1 0.1 pad_maximum_fusion.2
  37.3 0.2 fusion.63
  37.5 0.1 maximum_reduce_fusion.1
  37.6 0.2 fusion.61
  37.7 0.1 maximum_reduce_fusion
  37.8 0.2 fusion.59
  38.0 0.1 fusion.68
  38.2 0.4 fusion.64
  38.6 0.2 copy.26
  38.8 11.7 %all_to_all.30 = f32[2,16,8,256]{3,2,0,1:T(8,128)S(1)} all-to-all(f32[2,16,8,256]{3,2,0,1:T(8,128)S(1)} %copy.26), channel_id=1, replica_groups=mesh['freq'=8,'cell'=4] {'freq'}, dimensions={1} | all-to-all | bytes 524288 | tf_op jit(solution)/shard_map/all_to_all | solution.py:114
  50.5 1.2 %fusion = f32[2,64,600]{2,1,0:T(8,128)S(1)} fusion(f32[2,2,600,256]{3,2,1,0:T(8,128)S(1)} %copy-done, f32[2,2,8,8,256]{4,3,2,1,0:T(8,128)S(1)} %bitcast.106), kind=kOutput, calls=%fused_computation | convolution fusion | flops 235929600 | bytes 1667072 | tf_op jit(solution)/shard_map/kjm,ksm->kjs/dot_general | solution.py:69
  51.7 1.2 %fusion.2 = f32[2,64,600]{2,1,0:T(8,128)S(1)} fusion(f32[2,2,600,256]{3,2,1,0:T(8,128)S(1)} %copy-done, f32[2,2,8,8,256]{4,3,2,1,0:T(8,128)S(1)} %bitcast.107), kind=kOutput, calls=%fused_computation.2 | convolution fusion | flops 235929600 | bytes 1667072 | tf_op jit(solution)/shard_map/kjm,ksm->kjs/dot_general | solution.py:66
  52.9 1.2 %fusion.22 = f32[1,2,64,600]{3,2,1,0:T(8,128)S(1)} fusion(f32[2,64,600]{2,1,0:T(8,128)S(1)} %fusion, f32[2,2,600,256]{3,2,1,0:T(8,128)S(1)} %copy-done, f32[2,2,8,8,256]{4,3,2,1,0:T(8,128)S(1)} %bitcast.108), kind=kOutput, calls=%fused_computation.18 | convolution fusion | flops 236006400 | bytes 1994752 | tf_op jit(solution)/shard_map/kjm,ksm->kjs/dot_general | solution.py:69
  54.2 1.2 %fusion.25 = f32[1,2,64,600]{3,2,1,0:T(8,128)S(1)} fusion(f32[2,64,600]{2,1,0:T(8,128)S(1)} %fusion.2, f32[2,2,600,256]{3,2,1,0:T(8,128)S(1)} %copy-done, f32[2,2,8,8,256]{4,3,2,1,0:T(8,128)S(1)} %bitcast.109), kind=kOutput, calls=%fused_computation.19 | convolution fusion | flops 236006400 | bytes 1994752 | tf_op jit(solution)/shard_map/kjm,ksm->kjs/dot_general | solution.py:66
  55.4 0.9 pad_maximum_fusion
  56.3 33.7 %all-reduce.2.cloned.1.call-done = f32[2,2,64,600]{3,2,1,0:T(8,128)} async-done(((f32[2,2,64,600]{3,2,1,0:T(8,128)}), f32[2,2,64,600]{3,2,1,0:T(8,128)}) %all-reduce.2.cloned.1.call-update) | async-done | bytes 614416 | tf_op jit(solution)/shard_map/psum | solution.py:116
  90.1 1.6 %constant_dynamic-slice_fusion = f32[2,2,16,600]{3,2,1,0:T(8,128)} fusion(f32[2,2,64,600]{3,2,1,0:T(8,128)} %all-reduce.2.cloned.1.call-done, s32[]{:T(128)S(6)} %select_n.44), kind=kLoop, calls=%fused_computation.104 | loop fusion | bytes 307204 | tf_op jit(solution)/shard_map/dynamic_slice | solution.py:118
  (26 shorter events, 0.5 us)
Async XLA Ops:
  6.5 4.8 %copy-start = (f32[2,2,600,256]{3,2,1,0:T(8,128)S(1)}, f32[2,2,600,256]{3,2,1,0:T(8,128)}, u32[]{:S(2)}) copy-start(f32[2,2,600,256]{3,2,1,0:T(8,128)} %param.6) | copy-start | bytes 7372804
  6.5 4.8 %copy-start.1 = (f32[2,2,64,600]{3,2,1,0:T(8,128)S(1)}, f32[2,2,64,600]{3,2,1,0:T(8,128)}, u32[]{:S(2)}) copy-start(f32[2,2,64,600]{3,2,1,0:T(8,128)} %param.5) | copy-start | bytes 1843204
  11.3 10.2 %copy-start.2 = (s32[256]{0:T(256)S(1)}, s32[256]{0:T(256)}, u32[]{:S(2)}) copy-start(s32[256]{0:T(256)} %param.8) | copy-start | bytes 3076
  11.3 10.2 %copy-start.3 = (f32[8]{0:T(128)S(1)}, f32[8]{0:T(128)}, u32[]{:S(2)}) copy-start(f32[8]{0:T(128)} %param.9) | copy-start | bytes 100
  11.3 10.3 %copy-start.4 = (s32[64]{0:T(128)S(1)}, s32[64]{0:T(128)}, u32[]{:S(2)}) copy-start(s32[64]{0:T(128)} %param.7) | copy-start | bytes 772
  14.1 16.2 %all-to-all-start = ((f32[2,2,64,256]{3,1,0,2:T(2,128)}), f32[2,2,64,256]{3,1,0,2:T(2,128)S(1)}, u32[]{:S(2)}, u32[]{:S(2)}) async-start(f32[2,2,64,256]{3,1,0,2:T(2,128)} %copy.21), calls=%async_computation | async-start | bytes 524288 | tf_op jit(solution)/shard_map/all_to_all | solution.py:78
  21.4 68.7 %all-reduce.2.cloned.1.call-start = ((), (), s32[]{:S(2)}) async-start(), calls=%async_computation.2 | async-start | bytes 1310720 | tf_op jit(solution)/shard_map/psum | solution.py:116
  30.9 2.6 %collective-permute-start = (f32[121,4]{1,0:T(8,128)S(1)}, f32[121,4]{1,0:T(8,128)S(1)}, u32[]{:S(2)}, u32[]{:S(2)}) collective-permute-start(f32[121,4]{1,0:T(8,128)S(1)} %get-tuple-element.5), channel_id=1, source_target_pairs={{0,1},{1,2},{2,3},{4,5},{5,6},{6,7},{8,9},{9,10},{10,11},{12,13},{... | collective-permute-start | bytes 5816 | tf_op jit(solution)/shard_map/ppermute | solution.py:21
  32.2 4.9 %collective-permute-start.1 = (f32[121,4]{1,0:T(8,128)S(1)}, f32[121,4]{1,0:T(8,128)S(1)}, u32[]{:S(2)}, u32[]{:S(2)}) collective-permute-start(f32[121,4]{1,0:T(8,128)S(1)} %get-tuple-element.6), channel_id=1, source_target_pairs={{1,0},{2,1},{3,2},{5,4},{6,5},{7,6},{9,8},{10,9},{11,10},{13,12},{... | collective-permute-start | bytes 5816 | tf_op jit(solution)/shard_map/ppermute | solution.py:22
Sparse Core Ops, SparseCore 0:
  56.5 33.5 all-reduce.1
where the time goes:
time: 98.8 us; the launch traced here: 98.5 us
  waiting for transfers between devices  45.8 us (46%)
  between operations  13.7 us (14%)
  matrix products  12.1 us (12%)
  blocking collectives  11.7 us (12%)
  starting transfers between devices  9.93 us (10%)
  local copies, waits for them, and re-layouts  2.98 us (3%)
  other arithmetic  2.33 us (2%)
    psum x1, waiting for transfers between devices, on_device(): totals = lax.psum(partial_terms, 'cell')  33.7 us
    all_to_all x1, blocking collectives, on_device(): lax.all_to_all(spectrum, 'freq', split_axis=1, concat_axis=2, tiled=True)  11.7 us
    all_to_all x1, waiting for transfers between devices, on_device(): lax.all_to_all(local_spectrum, 'freq', split_axis=2, concat_axis=1, tiled...  8.46 us
    all_to_all x1, starting transfers between devices, on_device(): lax.all_to_all(local_spectrum, 'freq', split_axis=2, concat_axis=1, tiled...  7.31 us
    ppermute x1, waiting for transfers between devices, extended(): after = lax.ppermute(leading, axis, down)  3.54 us
    dot_general x1, matrix products, adjoint_product(): jnp.einsum('kjs,ksm->kjm', columns[0], blocks[1], precision=precise)  2.44 us
    dot_general x1, matrix products, adjoint_product(): jnp.einsum('kjs,ksm->kjm', columns[1], blocks[1], precision=precise)  2.3 us
  transfers between devices with their start and end apart: 4, of which 3 were waited for; matrix products, arithmetic and copies ran while one was open for 0% of the time, Pallas kernels for 0%

commit v1 on v0

--- a/solution.py
+++ b/solution.py
@@ -113,7 +113,7 @@
     spectrum = spectrum.reshape(2, freq_total, MODE_SHARE_WIDTH, C_DEV)
     returned = lax.all_to_all(spectrum, "freq", split_axis=1, concat_axis=2, tiled=True)
     partial_terms = forward_product(returned, freq_blocks)
-    totals = lax.psum(partial_terms, "cell")
+    totals = jnp.sum(lax.all_gather(partial_terms, "cell"), axis=0)
     share = col_total // lax.axis_size("cell")
     return lax.dynamic_slice_in_dim(totals, lax.axis_index("cell") * share, share, 2)
 

time: 98.8 us -> 91.4 us (0.925)
  waiting for transfers between devices: 45.8 us -> 37.3 us
  other arithmetic: 2.33 us -> 4.28 us
    psum x1 -> x0, waiting for transfers between devices: 33.7 us -> none  [on_device(): totals = lax.psum(partial_terms, 'cell')]
    all_gather x0 -> x1, waiting for transfers between devices: none -> 25.2 us  [on_device(): totals = jnp.sum(lax.all_gather(partial_terms, 'cell'), axis=0)]
    reduce_sum x0 -> x1, other arithmetic: none -> 1.97 us  [on_device(): totals = jnp.sum(lax.all_gather(partial_terms, 'cell'), axis=0)]
where the time goes in v1:
time: 91.4 us; the launch traced here: 91.1 us
  waiting for transfers between devices  37.3 us (41%)
  between operations  13.7 us (15%)
  matrix products  12.1 us (13%)
  blocking collectives  11.7 us (13%)
  starting transfers between devices  9.93 us (11%)
  other arithmetic  4.28 us (5%)
  local copies, waits for them, and re-layouts  2.07 us (2%)
    all_gather x1, waiting for transfers between devices, on_device(): totals = jnp.sum(lax.all_gather(partial_terms, 'cell'), axis=0)  25.2 us
    all_to_all x1, blocking collectives, on_device(): lax.all_to_all(spectrum, 'freq', split_axis=1, concat_axis=2, tiled=True)  11.7 us
    all_to_all x1, waiting for transfers between devices, on_device(): lax.all_to_all(local_spectrum, 'freq', split_axis=2, concat_axis=1, tiled...  8.46 us
    all_to_all x1, starting transfers between devices, on_device(): lax.all_to_all(local_spectrum, 'freq', split_axis=2, concat_axis=1, tiled...  7.31 us
    ppermute x1, waiting for transfers between devices, extended(): after = lax.ppermute(leading, axis, down)  3.54 us
    dot_general x1, matrix products, adjoint_product(): jnp.einsum('kjs,ksm->kjm', columns[0], blocks[1], precision=precise)  2.44 us
    dot_general x1, matrix products, adjoint_product(): jnp.einsum('kjs,ksm->kjm', columns[1], blocks[1], precision=precise)  2.3 us
    reduce_sum x1, other arithmetic, on_device(): totals = jnp.sum(lax.all_gather(partial_terms, 'cell'), axis=0)  1.97 us
  transfers between devices with their start and end apart: 4, of which 3 were waited for; matrix products, arithmetic and copies ran while one was open for 0% of the time, Pallas kernels for 0%

profile of v1, /device:TPU:0, one launch (start us, length us, event | category | flops | bytes accessed | tf_op | source)
XLA Modules:
  0.0 91.1 jit_solution(17092615549608225209)
XLA Ops:
  6.5 2.4 %fusion.4 = f32[2,64,256]{2,1,0:T(8,128)S(1)} fusion(f32[2,2,600,256]{3,2,1,0:T(8,128)} %param.6, f32[2,2,64,600]{3,2,1,0:T(8,128)} %param.5), kind=kOutput, calls=%fused_computation.4 | convolution fusion | flops 235929600 | bytes 1687552 | tf_op jit(solution)/shard_map/kjs,ksm->kjm/dot_general | solution.py:59
  9.0 2.3 %fusion.6 = f32[2,64,256]{2,1,0:T(8,128)S(1)} fusion(f32[2,2,600,256]{3,2,1,0:T(8,128)} %param.6, f32[2,2,64,600]{3,2,1,0:T(8,128)} %param.5), kind=kOutput, calls=%fused_computation.6 | convolution fusion | flops 235929600 | bytes 1687552 | tf_op jit(solution)/shard_map/kjs,ksm->kjm/dot_general | solution.py:56
  11.4 0.9 fusion.37
  12.3 0.9 fusion.31
  13.2 0.9 copy.21
  14.1 7.3 %all-to-all-start = ((f32[2,2,64,256]{3,1,0,2:T(2,128)}), f32[2,2,64,256]{3,1,0,2:T(2,128)S(1)}, u32[]{:S(2)}, u32[]{:S(2)}) async-start(f32[2,2,64,256]{3,1,0,2:T(2,128)} %copy.21), calls=%async_computation | async-start | bytes 524288 | tf_op jit(solution)/shard_map/all_to_all | solution.py:78
  21.6 0.1 select_reduce_fusion
  21.9 8.5 %all-to-all-done = f32[2,2,64,256]{3,1,0,2:T(2,128)S(1)} async-done(((f32[2,2,64,256]{3,1,0,2:T(2,128)}), f32[2,2,64,256]{3,1,0,2:T(2,128)S(1)}, u32[]{:S(2)}, u32[]{:S(2)}) %all-to-all-start) | async-done | bytes 262176 | tf_op jit(solution)/shard_map/all_to_all | solution.py:78
  30.4 0.3 convolution_select_fusion
  30.8 0.1 fusion.69
  30.9 1.3 %collective-permute-start = (f32[121,4]{1,0:T(8,128)S(1)}, f32[121,4]{1,0:T(8,128)S(1)}, u32[]{:S(2)}, u32[]{:S(2)}) collective-permute-start(f32[121,4]{1,0:T(8,128)S(1)} %get-tuple-element.5), channel_id=1, source_target_pairs={{0,1},{1,2},{2,3},{4,5},{5,6},{6,7},{8,9},{9,10},{10,11},{12,13},{... | collective-permute-start | bytes 5816 | tf_op jit(solution)/shard_map/ppermute | solution.py:21
  32.2 1.3 %collective-permute-start.1 = (f32[121,4]{1,0:T(8,128)S(1)}, f32[121,4]{1,0:T(8,128)S(1)}, u32[]{:S(2)}, u32[]{:S(2)}) collective-permute-start(f32[121,4]{1,0:T(8,128)S(1)} %get-tuple-element.6), channel_id=1, source_target_pairs={{1,0},{2,1},{3,2},{5,4},{6,5},{7,6},{9,8},{10,9},{11,10},{13,12},{... | collective-permute-start | bytes 5816 | tf_op jit(solution)/shard_map/ppermute | solution.py:22
  33.5 3.5 %collective-permute-done.1 = f32[121,4]{1,0:T(8,128)S(1)} collective-permute-done((f32[121,4]{1,0:T(8,128)S(1)}, f32[121,4]{1,0:T(8,128)S(1)}, u32[]{:S(2)}, u32[]{:S(2)}) %collective-permute-start.1) | collective-permute-done | bytes 1968 | tf_op jit(solution)/shard_map/ppermute | solution.py:22
  37.1 0.1 maximum_reduce_fusion.2
  37.1 0.1 pad_maximum_fusion.2
  37.3 0.2 fusion.63
  37.5 0.1 maximum_reduce_fusion.1
  37.6 0.2 fusion.61
  37.7 0.1 maximum_reduce_fusion
  37.8 0.2 fusion.59
  38.0 0.1 fusion.68
  38.2 0.4 fusion.64
  38.6 0.2 copy.26
  38.8 11.7 %all_to_all.30 = f32[2,16,8,256]{3,2,0,1:T(8,128)S(1)} all-to-all(f32[2,16,8,256]{3,2,0,1:T(8,128)S(1)} %copy.26), channel_id=1, replica_groups=mesh['freq'=8,'cell'=4] {'freq'}, dimensions={1} | all-to-all | bytes 524288 | tf_op jit(solution)/shard_map/all_to_all | solution.py:114
  50.5 1.2 %fusion = f32[2,64,600]{2,1,0:T(8,128)S(1)} fusion(f32[2,2,600,256]{3,2,1,0:T(8,128)S(1)} %copy-done, f32[2,2,8,8,256]{4,3,2,1,0:T(8,128)S(1)} %bitcast.108), kind=kOutput, calls=%fused_computation | convolution fusion | flops 235929600 | bytes 1667072 | tf_op jit(solution)/shard_map/kjm,ksm->kjs/dot_general | solution.py:69
  51.7 1.2 %fusion.2 = f32[2,64,600]{2,1,0:T(8,128)S(1)} fusion(f32[2,2,600,256]{3,2,1,0:T(8,128)S(1)} %copy-done, f32[2,2,8,8,256]{4,3,2,1,0:T(8,128)S(1)} %bitcast.109), kind=kOutput, calls=%fused_computation.2 | convolution fusion | flops 235929600 | bytes 1667072 | tf_op jit(solution)/shard_map/kjm,ksm->kjs/dot_general | solution.py:66
  52.9 1.2 %fusion.22 = f32[1,2,64,600]{3,2,1,0:T(8,128)S(1)} fusion(f32[2,64,600]{2,1,0:T(8,128)S(1)} %fusion, f32[2,2,600,256]{3,2,1,0:T(8,128)S(1)} %copy-done, f32[2,2,8,8,256]{4,3,2,1,0:T(8,128)S(1)} %bitcast.110), kind=kOutput, calls=%fused_computation.18 | convolution fusion | flops 236006400 | bytes 1994752 | tf_op jit(solution)/shard_map/kjm,ksm->kjs/dot_general | solution.py:69
  54.2 1.2 %fusion.25 = f32[1,2,64,600]{3,2,1,0:T(8,128)S(1)} fusion(f32[2,64,600]{2,1,0:T(8,128)S(1)} %fusion.2, f32[2,2,600,256]{3,2,1,0:T(8,128)S(1)} %copy-done, f32[2,2,8,8,256]{4,3,2,1,0:T(8,128)S(1)} %bitcast.111), kind=kOutput, calls=%fused_computation.19 | convolution fusion | flops 236006400 | bytes 1994752 | tf_op jit(solution)/shard_map/kjm,ksm->kjs/dot_general | solution.py:66
  55.4 0.9 pad_maximum_fusion
  56.3 25.2 %all-gather.3.cloned.1.call-done = f32[8,2,64,600]{3,2,1,0:T(8,128)} async-done(((f32[2,2,64,600]{3,2,1,0:T(8,128)}), f32[8,2,64,600]{3,2,1,0:T(8,128)}) %all-gather.3.cloned.1.call-update) | async-done | bytes 2457616 | tf_op jit(solution)/shard_map/all_gather | solution.py:116
  81.6 2.0 %reduce_sum.19 = f32[2,2,64,600]{3,2,1,0:T(8,128)S(1)} reduce(f32[4,2,2,64,600]{4,3,2,1,0:T(8,128)} %bitcast.107, f32[]{:T(128)} %constant.27.clone.1), dimensions={0}, to_apply=%region_1.2 | reduce | flops 460800 | bytes 3072004 | tf_op jit(solution)/shard_map/reduce_sum | solution.py:116
  83.5 0.7 constant_dynamic-slice_fusion
  (27 shorter events, 0.6 us)
Async XLA Ops:
  6.5 4.8 %copy-start = (f32[2,2,600,256]{3,2,1,0:T(8,128)S(1)}, f32[2,2,600,256]{3,2,1,0:T(8,128)}, u32[]{:S(2)}) copy-start(f32[2,2,600,256]{3,2,1,0:T(8,128)} %param.6) | copy-start | bytes 7372804
  6.5 4.8 %copy-start.1 = (f32[2,2,64,600]{3,2,1,0:T(8,128)S(1)}, f32[2,2,64,600]{3,2,1,0:T(8,128)}, u32[]{:S(2)}) copy-start(f32[2,2,64,600]{3,2,1,0:T(8,128)} %param.5) | copy-start | bytes 1843204
  11.3 10.2 %copy-start.2 = (s32[256]{0:T(256)S(1)}, s32[256]{0:T(256)}, u32[]{:S(2)}) copy-start(s32[256]{0:T(256)} %param.8) | copy-start | bytes 3076
  11.3 10.2 %copy-start.3 = (f32[8]{0:T(128)S(1)}, f32[8]{0:T(128)}, u32[]{:S(2)}) copy-start(f32[8]{0:T(128)} %param.9) | copy-start | bytes 100
  11.3 10.3 %copy-start.4 = (s32[64]{0:T(128)S(1)}, s32[64]{0:T(128)}, u32[]{:S(2)}) copy-start(s32[64]{0:T(128)} %param.7) | copy-start | bytes 772
  14.1 16.2 %all-to-all-start = ((f32[2,2,64,256]{3,1,0,2:T(2,128)}), f32[2,2,64,256]{3,1,0,2:T(2,128)S(1)}, u32[]{:S(2)}, u32[]{:S(2)}) async-start(f32[2,2,64,256]{3,1,0,2:T(2,128)} %copy.21), calls=%async_computation | async-start | bytes 524288 | tf_op jit(solution)/shard_map/all_to_all | solution.py:78
  21.4 60.2 %all-gather.3.cloned.1.call-start = ((), (), s32[]{:S(2)}) async-start(), calls=%async_computation.2 | async-start | bytes 3276800 | tf_op jit(solution)/shard_map/all_gather | solution.py:116
  30.9 2.6 %collective-permute-start = (f32[121,4]{1,0:T(8,128)S(1)}, f32[121,4]{1,0:T(8,128)S(1)}, u32[]{:S(2)}, u32[]{:S(2)}) collective-permute-start(f32[121,4]{1,0:T(8,128)S(1)} %get-tuple-element.5), channel_id=1, source_target_pairs={{0,1},{1,2},{2,3},{4,5},{5,6},{6,7},{8,9},{9,10},{10,11},{12,13},{... | collective-permute-start | bytes 5816 | tf_op jit(solution)/shard_map/ppermute | solution.py:21
  32.2 4.9 %collective-permute-start.1 = (f32[121,4]{1,0:T(8,128)S(1)}, f32[121,4]{1,0:T(8,128)S(1)}, u32[]{:S(2)}, u32[]{:S(2)}) collective-permute-start(f32[121,4]{1,0:T(8,128)S(1)} %get-tuple-element.6), channel_id=1, source_target_pairs={{1,0},{2,1},{3,2},{5,4},{6,5},{7,6},{9,8},{10,9},{11,10},{13,12},{... | collective-permute-start | bytes 5816 | tf_op jit(solution)/shard_map/ppermute | solution.py:22
Sparse Core Ops, SparseCore 0:
  56.4 25.0 all-gather.2
